TPU v7x, 32 devices: a whole 2x2x4 slice. The times are simulated.
32 devices in a mesh: cfg: 2 (over y), ta: 4 (over z), sa: 2 (over x), src: 2 (over core).
Axes of the slice: x: 2, y: 2, z: 4, core: 2. Of those that a mesh axis runs over, the one named last changes fastest.
Arguments:
- prop: bfloat16 [4, 8, 2, 12, 12, 512], P(('cfg', 'src'), 'ta', None, None, None, 'sa'), parts along dimension 0, may hold values from -6 to 6
- eps_rows: int32 [24, 3], replicated, may hold values from 0 to 11
- eps_sign: int32 [24], replicated, may hold values from 0 to 1
- source_sites: int32 [4, 3], P('cfg'), parts along dimension 0, may hold values from 0 to 15, as said below
- momenta: int32 [8, 3], replicated, may hold values from -2 to 2
Outputs:
- blocks: float32 [4, 8, 2, 8, 1728], P('cfg', None, None, 'ta', 'sa'), parts along dimension 0
There are 2 independent parts, one for each index of `cfg`. A program takes and returns all parts, laid end to end along the dimension named above; an argument that names none is the same for every part. Nothing has to cross between parts.
Inputs may be any that keep to these rules, and one draw needn't show every extreme that they name: `source_sites`: each row is a lattice site: first coordinate below 2, second below 16, third below 16.
All inputs are finite; a program needn't handle non-finite values.
Results may differ from a plain program's by a relative error of at most 0.0045.
Values sent between devices are 32-bit elements; how exact they have to be, the bound alone decides.
No kernel may reach another device: no remote copies, remote signals or barrier semaphores. Data moves between devices by JAX's collectives and lax.ppermute only.
A program may use at most 128 MiB of HBM per device.

v0:
```python
import math

import jax
import jax.numpy as jnp
from jax import lax
from jax.sharding import PartitionSpec as P

LY = 16
LZ = 16


def phase_table(position, momenta, site_index, extent_x):
    coord_x = site_index // (LY * LZ)
    coord_y = site_index // LZ % LY
    coord_z = site_index % LZ
    part_x = momenta[:, 0:1] * (coord_x[None, :] - position[0]) % extent_x
    part_y = momenta[:, 1:2] * (coord_y[None, :] - position[1]) % LY
    part_z = momenta[:, 2:3] * (coord_z[None, :] - position[2]) % LZ
    angle = (
        2.0
        * math.pi
        * (
            part_x.astype(jnp.float32) / extent_x
            + part_y.astype(jnp.float32) / LY
            + part_z.astype(jnp.float32) / LZ
        )
    )
    return jnp.concatenate([jnp.cos(angle), jnp.sin(angle)], axis=0).astype(jnp.bfloat16)


def contract(slab, rows, weights):
    first = jnp.take(slab, rows[:, 0], axis=1).astype(jnp.float32)
    second = jnp.take(slab, rows[:, 1], axis=1).astype(jnp.float32)
    third = jnp.take(slab, rows[:, 2], axis=1)
    scaled = weights[:, None, None, None]
    real = scaled * (
        first[0][:, :, None] * second[0][:, None] - first[1][:, :, None] * second[1][:, None]
    )
    imag = scaled * (
        first[0][:, :, None] * second[1][:, None] + first[1][:, :, None] * second[0][:, None]
    )
    pair = jnp.stack([real, imag]).astype(jnp.bfloat16)
    mixer = jnp.stack([jnp.stack([third[0], -third[1]]), jnp.stack([third[1], third[0]])])
    block = jnp.einsum("ceijx,oceLx->oijLx", pair, mixer, preferred_element_type=jnp.float32)
    width = slab.shape[1]
    return block.astype(jnp.bfloat16).reshape(2 * width * width * width, slab.shape[-1])


def mix_phase(table, quark):
    product = lax.dot_general(
        table, quark, (((1,), (1,)), ((), ())), preferred_element_type=jnp.float32
    )
    half_m = table.shape[0] // 2
    half_k = quark.shape[0] // 2
    cos_re = product[:half_m, :half_k]
    cos_im = product[:half_m, half_k:]
    sin_re = product[half_m:, :half_k]
    sin_im = product[half_m:, half_k:]
    return jnp.stack([cos_re + sin_im, cos_im - sin_re])


def per_device(prop, eps_rows, eps_sign, source_sites, momenta):
    src_count = prop.shape[0]
    time_count = prop.shape[1]
    width = prop.shape[3]
    site_count = prop.shape[5]
    sites_total = site_count * lax.axis_size("sa")
    extent_x = sites_total // (LY * LZ)
    site_index = lax.axis_index("sa") * site_count + jnp.arange(site_count, dtype=jnp.int32)
    weights = (2 * eps_sign - 1).astype(jnp.float32)
    scale = 1.0 / math.sqrt(4.0 * eps_rows.shape[0] * sites_total)
    first_source = lax.axis_index("src") * src_count
    positions = lax.dynamic_slice_in_dim(source_sites, first_source, src_count, 0)
    tables = jnp.stack([phase_table(positions[0], momenta, site_index, extent_x)])
    slabs = prop.reshape((src_count * time_count,) + prop.shape[2:])
    owners = jnp.repeat(jnp.arange(src_count, dtype=jnp.int32), time_count)

    def project(items):
        slab, owner = items
        quark = contract(slab, eps_rows, weights)
        return scale * mix_phase(tables[owner], quark)

    partial_value = lax.map(project, (slabs, owners))
    partial_value = partial_value.reshape(
        src_count, time_count, 2, momenta.shape[0], width * width * width
    )
    summed = lax.psum_scatter(partial_value, "sa", scatter_dimension=4, tiled=True)
    finished = lax.all_to_all(summed, "ta", split_axis=3, concat_axis=1, tiled=True)
    return lax.all_gather(finished, "src", axis=0, tiled=True)


def solution(mesh):
    return jax.shard_map(
        per_device,
        mesh=mesh,
        in_specs=(P(("cfg", "src"), "ta", None, None, None, "sa"), P(), P(), P("cfg", None), P()),
        out_specs=P("cfg", None, None, "ta", "sa"),
        check_vma=False,
    )
```

profile of v0, /device:TPU:0, one launch (start us, length us, event | category | flops | bytes accessed | tf_op | source)
XLA Modules:
  0.0 323.2 jit_solution(15552078244908661821)
XLA Ops:
  6.5 0.7 copy-done
  7.2 0.7 fusion.27
  7.9 0.8 slice_bitcast_fusion.2
  8.7 1.1 add_convert_fusion
  9.8 0.7 fusion.24
  10.5 1.3 fusion.20
  11.8 0.1 fusion.18
  11.9 257.3 %while.10 = (s32[]{:T(128)}, f32[2,2,8,1728]{3,2,1,0:T(8,128)}, bf16[2,2,12,12,256]{4,1,3,2,0:T(2,128)(2,1)}, s32[24,3]{0,1:T(4,128)}, f32[24]{0:T(128)}, /*index=5*/bf16[1,16,256]{2,1,0:T(8,128)(2,1)S(1)}, s32[]{:T(128)}) while((s32[]{:T(128)}, f32[2,2,8,1728]{3,2,1,0:T(8,128)}, bf16[2,2,12,12,256]{4,1,3,2,0:T(2,128)(2,1)}, ...), condition=%wide.region_1.3_spmd, body=%wide.region_0.2_spmd.sunk | while | flops 126235056 | bytes 50939416 | solution.py:83
  12.0 1.3 compare_and_fusion.4
  13.3 1.0 dynamic-slice_bitcast_fusion.2
  14.3 1.1 gather_fusion.1
  15.5 1.1 gather_fusion.2
  16.6 0.6 bitcast_convert_fusion.4
  17.2 0.5 fusion.46
  17.7 0.1 copy.79
  17.8 0.5 fusion.47
  18.2 0.1 copy.80
  18.3 0.1 copy.81
  18.4 1.8 multiply_convert_fusion.3
  20.3 0.3 maximum_bitcast_fusion.9
  20.6 34.0 %copy.83 = bf16[2,24,12,12,256,1]{1,3,0,2,5,4:T(8,128)(2,1)} copy(bf16[2,24,12,12,256,1]{4,1,3,2,0,5:T(8,128)(2,1)S(1)} %maximum_bitcast_fusion.9) | data formatting | bytes 7077888 | tf_op jit(solution)/shard_map/while/body/eval_jaxpr/stack | solution.py:42
  54.6 2.1 gather_fusion
  56.7 1.0 fusion.45
  57.6 0.7 slice_negate_fusion.2
  58.7 6.5 %copy.78 = bf16[2,2,24,12,256,1]{2,3,1,5,0,4:T(8,128)(2,1)} copy(bf16[2,2,24,12,256,1]{4,2,3,1,0,5:T(8,128)(2,1)S(1)} %maximum_bitcast_fusion.8) | data formatting | bytes 1179648 | tf_op jit(solution)/shard_map/while/body/eval_jaxpr/stack | solution.py:43
  65.2 41.2 %fusion.48 = bf16[2,12,12,12,256]{2,3,1,0,4:T(8,128)(2,1)} fusion(bf16[2,2,24,12,256,1]{2,3,1,5,0,4:T(8,128)(2,1)} %copy.78, bf16[2,24,12,12,256,1]{1,3,0,2,5,4:T(8,128)(2,1)} %copy.83), kind=kOutput, calls=%fused_computation.4.clone.1 | convolution fusion | flops 85819392 | bytes 5898240 | tf_op jit(solution)/shard_map/while/body/eval_jaxpr/ceijx,oceLx->oijLx/dot_general | solution.py:44
  106.4 29.3 %copy.84 = bf16[2,12,12,12,256]{4,3,2,1,0:T(8,128)(2,1)S(1)} copy(bf16[2,12,12,12,256]{2,3,1,0,4:T(8,128)(2,1)} %fusion.48) | data formatting | bytes 3538944 | tf_op jit(solution)/shard_map/while/body/eval_jaxpr/convert_element_type | solution.py:46
  135.7 2.0 reshape.465
  137.7 2.0 convolution_bitcast_fusion.2
  139.7 0.1 fusion.49
  139.9 0.7 copy-done.4
  140.6 1.3 compare_and_fusion.4
  141.9 1.0 dynamic-slice_bitcast_fusion.2
  142.9 1.1 gather_fusion.1
  144.1 1.1 gather_fusion.2
  145.3 0.6 bitcast_convert_fusion.4
  145.9 0.5 fusion.46
  146.3 0.1 copy.79
  146.4 0.5 fusion.47
  146.9 0.1 copy.80
  146.9 0.1 copy.81
  147.1 1.8 multiply_convert_fusion.3
  148.9 0.3 maximum_bitcast_fusion.9
  149.2 34.0 %copy.83 = bf16[2,24,12,12,256,1]{1,3,0,2,5,4:T(8,128)(2,1)} copy(bf16[2,24,12,12,256,1]{4,1,3,2,0,5:T(8,128)(2,1)S(1)} %maximum_bitcast_fusion.9) | data formatting | bytes 7077888 | tf_op jit(solution)/shard_map/while/body/eval_jaxpr/stack | solution.py:42
  183.2 2.1 gather_fusion
  185.3 1.0 fusion.45
  186.3 0.7 slice_negate_fusion.2
  187.3 6.5 %copy.78 = bf16[2,2,24,12,256,1]{2,3,1,5,0,4:T(8,128)(2,1)} copy(bf16[2,2,24,12,256,1]{4,2,3,1,0,5:T(8,128)(2,1)S(1)} %maximum_bitcast_fusion.8) | data formatting | bytes 1179648 | tf_op jit(solution)/shard_map/while/body/eval_jaxpr/stack | solution.py:43
  193.8 41.2 %fusion.48 = bf16[2,12,12,12,256]{2,3,1,0,4:T(8,128)(2,1)} fusion(bf16[2,2,24,12,256,1]{2,3,1,5,0,4:T(8,128)(2,1)} %copy.78, bf16[2,24,12,12,256,1]{1,3,0,2,5,4:T(8,128)(2,1)} %copy.83), kind=kOutput, calls=%fused_computation.4.clone.1 | convolution fusion | flops 85819392 | bytes 5898240 | tf_op jit(solution)/shard_map/while/body/eval_jaxpr/ceijx,oceLx->oijLx/dot_general | solution.py:44
  235.0 29.3 %copy.84 = bf16[2,12,12,12,256]{4,3,2,1,0:T(8,128)(2,1)S(1)} copy(bf16[2,12,12,12,256]{2,3,1,0,4:T(8,128)(2,1)} %fusion.48) | data formatting | bytes 3538944 | tf_op jit(solution)/shard_map/while/body/eval_jaxpr/convert_element_type | solution.py:46
  264.3 2.0 reshape.465
  266.3 2.0 convolution_bitcast_fusion.2
  268.3 0.1 fusion.49
  268.5 0.7 copy-done.4
  269.2 4.4 %copy.54 = f32[1,2,2,8,1728]{3,2,1,0,4:T(2,128)S(1)} copy(f32[1,2,2,8,1728]{4,3,2,1,0:T(8,128)} %bitcast.122) | data formatting | bytes 442368
  273.6 3.5 %reshape.450 = f32[1728,32]{1,0:T(8,128)} reshape(f32[1728,1,2,2,8]{4,3,2,1,0:T(2,128)S(1)} %bitcast.118) | data formatting | bytes 442368
  277.2 21.5 %reduce-scatter.4.cloned.1.call-done = f32[864,32]{1,0:T(8,128)} async-done(((f32[1728,32]{1,0:T(8,128)}), f32[864,32]{1,0:T(8,128)}) %reduce-scatter.4.cloned.1.call-update) | async-done | bytes 110608
  298.6 2.7 reshape.451
  301.3 1.8 copy.44
  303.2 10.3 %all_to_all.18 = f32[1,2,2,8,864]{4,2,1,0,3:T(2,128)S(1)} all-to-all(f32[1,2,2,8,864]{4,2,1,0,3:T(2,128)S(1)} %copy.44), channel_id=1, replica_groups=mesh['cfg'=2,'ta'=4,'sa'=2,'src'=2] {'ta'}, dimensions={3} | all-to-all | bytes 221184 | tf_op jit(solution)/shard_map/all_to_all | solution.py:88
  313.5 0.1 copy.45
  313.5 0.1 all_to_all.16
  313.6 2.0 all_gather.3
  315.6 0.8 copy.46
  (38 shorter events, 0.7 us)
Async XLA Ops:
  6.5 0.7 copy-start
  6.5 292.1 %reduce-scatter.4.cloned.1.call-start = ((), (), s32[]{:S(2)}) async-start(), calls=%async_computation.2 | async-start | bytes 1327104
  14.3 4.1 %copy-start.2 = (bf16[2,12,12,256]{3,0,2,1:T(2,128)(2,1)}, bf16[2,12,12,256]{3,0,2,1:T(2,128)(2,1)S(1)}, u32[]{:S(2)}) copy-start(bf16[2,12,12,256]{3,0,2,1:T(2,128)(2,1)S(1)} %dynamic-slice_bitcast_fusion.2) | copy-start | bytes 442372 | tf_op jit(solution)/shard_map/while
  135.7 4.1 %copy-start.3 = (f32[2,2,8,1728]{3,2,1,0:T(8,128)S(1)}, f32[2,2,8,1728]{3,2,1,0:T(8,128)}, u32[]{:S(2)}) copy-start(f32[2,2,8,1728]{3,2,1,0:T(8,128)} %get-tuple-element.173) | copy-start | bytes 663556 | tf_op jit(solution)/shard_map/while
  139.9 0.7 copy-start.4
  142.9 4.1 %copy-start.2 = (bf16[2,12,12,256]{3,0,2,1:T(2,128)(2,1)}, bf16[2,12,12,256]{3,0,2,1:T(2,128)(2,1)S(1)}, u32[]{:S(2)}) copy-start(bf16[2,12,12,256]{3,0,2,1:T(2,128)(2,1)S(1)} %dynamic-slice_bitcast_fusion.2) | copy-start | bytes 442372 | tf_op jit(solution)/shard_map/while
  264.3 4.1 %copy-start.3 = (f32[2,2,8,1728]{3,2,1,0:T(8,128)S(1)}, f32[2,2,8,1728]{3,2,1,0:T(8,128)}, u32[]{:S(2)}) copy-start(f32[2,2,8,1728]{3,2,1,0:T(8,128)} %get-tuple-element.173) | copy-start | bytes 663556 | tf_op jit(solution)/shard_map/while
  268.5 0.7 copy-start.4
  273.6 42.8 %copy-start.1 = (s32[2,3]{1,0:T(2,128)S(1)}, s32[2,3]{1,0:T(2,128)}, u32[]{:S(2)}) copy-start(s32[2,3]{1,0:T(2,128)} %param.12) | copy-start | bytes 76
Sparse Core Ops, SparseCore 0:
  277.3 21.2 reduce-scatter.3
where the time goes:
time: 325 us; the launch traced here: 323 us
  local copies, waits for them, and re-layouts  174 us (54%)
  matrix products  86.5 us (27%)
  waiting for transfers between devices  21.5 us (7%)
  other arithmetic  15.3 us (5%)
  between operations  13.5 us (4%)
  blocking collectives  12.3 us (4%)
    dot_general x2, matrix products, contract(): jnp.einsum('ceijx,oceLx->oijLx', pair, mixer, preferred_element_type=jnp....  82.4 us
    another operation x2, local copies, waits for them, and re-layouts, contract(): pair = jnp.stack([real, imag]).astype(jnp.bfloat16)  68 us
    convert_element_type x2, local copies, waits for them, and re-layouts, contract(): block.astype(jnp.bfloat16)  58.5 us
    unnamed x2, waiting for transfers between devices  21.5 us
    another operation x2, local copies, waits for them, and re-layouts, contract(): jnp.stack([jnp.stack([third[0], -third[1]]), jnp.stack([third[1], third[0...  13.1 us
    unnamed x7, local copies, waits for them, and re-layouts  11.3 us
    all_to_all x1, blocking collectives, per_device(): lax.all_to_all(summed, 'ta', split_axis=3, concat_axis=1, tiled=True)  10.3 us
  transfers between devices with their start and end apart: 1, of which 1 were waited for; matrix products, arithmetic and copies ran while one was open for 0% of the time, Pallas kernels for 0%

commit v1 on v0

v1 whole, which is shorter than its diff:
```python
import math

import jax
import jax.numpy as jnp
from jax import lax
from jax.experimental import pallas as pl
from jax.experimental.pallas import tpu as pltpu
from jax.sharding import PartitionSpec as P

LY = 16
LZ = 16
GROUP = 4


def wrap(value, length):
    if length & (length - 1) == 0:
        return value & (length - 1)
    return jnp.mod(value, length)


def project_kernel(rows, signs, sites, momenta, prop, out, spread, tiled, phased, pairs, total, *,
                   times, site_count, sites_total, scale):
    step = pl.program_id(0)
    width = prop.shape[2]
    mom = momenta.shape[0]
    terms = rows.shape[0]
    extent_x = sites_total // (LY * LZ)
    per = mom * width
    square = width * width

    owner = lax.axis_index("src") * (pl.num_programs(0) // times) + step // times
    site = lax.axis_index("sa") * site_count + lax.broadcasted_iota(jnp.int32, (mom, site_count), 1)
    coord_x = site // (LY * LZ)
    coord_y = wrap(site // LZ, LY)
    coord_z = wrap(site, LZ)
    part_x = wrap(momenta[:, 0:1] * (coord_x - sites[owner, 0]), extent_x)
    part_y = wrap(momenta[:, 1:2] * (coord_y - sites[owner, 1]), LY)
    part_z = wrap(momenta[:, 2:3] * (coord_z - sites[owner, 2]), LZ)
    angle = (2.0 * math.pi) * (
        part_x.astype(jnp.float32) / extent_x
        + part_y.astype(jnp.float32) / LY
        + part_z.astype(jnp.float32) / LZ
    )
    cosine = jnp.cos(angle).astype(jnp.bfloat16).astype(jnp.float32)
    sine = jnp.sin(angle).astype(jnp.bfloat16).astype(jnp.float32)
    low = lax.broadcasted_iota(jnp.int32, (8, site_count), 0) < 4

    def prepare(r, carry):
        parts = [prop[0, c, r].astype(jnp.float32) for c in range(2)]
        for c in range(2):
            tiled[r, c] = jnp.concatenate([parts[c], parts[c]], axis=0)
            for j in range(0, width, 2):
                first = jnp.broadcast_to(parts[c][j:j + 1], (8, site_count))
                second = jnp.broadcast_to(parts[c][j + 1:j + 2], (8, site_count))
                at = j * width
                spread[r, c, at:at + 8] = first
                spread[r, c, at + 8:at + 16] = jnp.where(low, first, second)
                spread[r, c, at + 16:at + 24] = second
        for i in range(0, width, 2):
            reals = []
            imags = []
            for q in (i, i + 1):
                re = jnp.broadcast_to(parts[0][q:q + 1], (mom, site_count))
                im = jnp.broadcast_to(parts[1][q:q + 1], (mom, site_count))
                reals.append(re * cosine + im * sine)
                imags.append(im * cosine - re * sine)
            real = jnp.concatenate(reals, axis=0).astype(jnp.bfloat16)
            imag = jnp.concatenate(imags, axis=0)
            minus = (-imag).astype(jnp.bfloat16)
            imag = imag.astype(jnp.bfloat16)
            at = i * mom
            phased[r, at:at + 2 * mom, :site_count] = real
            phased[r, at:at + 2 * mom, site_count:] = minus
            phased[r, per + at:per + at + 2 * mom, :site_count] = imag
            phased[r, per + at:per + at + 2 * mom, site_count:] = real
        return carry

    lax.fori_loop(0, width, prepare, 0)
    total[...] = jnp.zeros_like(total)

    def accumulate(block, carry):
        left = []
        for u in range(GROUP):
            e = block * GROUP + u
            r1 = rows[e, 1]
            r2 = rows[e, 2]
            weight = (2 * signs[e] - 1).astype(jnp.float32)
            re2 = tiled[r2, 0] * weight
            im2 = tiled[r2, 1] * weight
            re2 = jnp.concatenate([re2, re2], axis=0)
            im2 = jnp.concatenate([im2, im2], axis=0)
            at = u * 2 * site_count
            for j in range(0, square, 4 * width):
                re1 = spread[r1, 0, j:j + 4 * width]
                im1 = spread[r1, 1, j:j + 4 * width]
                pairs[j:j + 4 * width, at:at + site_count] = (re1 * re2 - im1 * im2).astype(jnp.bfloat16)
                pairs[j:j + 4 * width, at + site_count:at + 2 * site_count] = (
                    re1 * im2 + im1 * re2
                ).astype(jnp.bfloat16)
            left.append(phased[rows[e, 0]])
        total[...] += lax.dot_general(
            jnp.concatenate(left, axis=1), pairs[...], (((1,), (1,)), ((), ())),
            preferred_element_type=jnp.float32,
        )
        return carry

    lax.fori_loop(0, terms // GROUP, accumulate, 0)

    owners = out.shape[0]
    mine = out.shape[3]
    span = out.shape[4] // square
    halves = width // span
    for c in range(2):
        for i in range(width):
            value = total[c * per + i * mom:c * per + (i + 1) * mom] * scale
            half = i // span
            at = (i % span) * square
            for a in range(owners // halves):
                out[a * halves + half, 0, c, :, at:at + square] = value[a * mine:(a + 1) * mine]


def per_device(prop, eps_rows, eps_sign, source_sites, momenta):
    src_count, time_count = prop.shape[:2]
    width = prop.shape[3]
    site_count = prop.shape[5]
    sites_total = site_count * lax.axis_size("sa")
    mom = momenta.shape[0]
    terms = eps_rows.shape[0]
    scale = 1.0 / math.sqrt(4.0 * terms * sites_total)
    slabs = prop.reshape((src_count * time_count,) + prop.shape[2:])
    owners = lax.axis_size("ta") * lax.axis_size("sa")
    mine = mom // lax.axis_size("ta")
    span = width ** 3 // lax.axis_size("sa")

    def body(*refs):
        project_kernel(*refs, times=time_count, site_count=site_count, sites_total=sites_total, scale=scale)

    smem = pl.BlockSpec(memory_space=pltpu.SMEM)
    partial_value = pl.pallas_call(
        body,
        grid=(slabs.shape[0],),
        in_specs=[
            smem, smem, smem,
            pl.BlockSpec(momenta.shape, lambda s: (0, 0)),
            pl.BlockSpec((1,) + slabs.shape[1:], lambda s: (s, 0, 0, 0, 0)),
        ],
        out_specs=pl.BlockSpec((owners, 1, 2, mine, span), lambda s: (0, s, 0, 0, 0)),
        out_shape=jax.ShapeDtypeStruct((owners, slabs.shape[0], 2, mine, span), jnp.float32),
        scratch_shapes=[
            pltpu.VMEM((width, 2, width * width, site_count), jnp.float32),
            pltpu.VMEM((width, 2, 2 * width, site_count), jnp.float32),
            pltpu.VMEM((width, 2 * width * mom, 2 * site_count), jnp.bfloat16),
            pltpu.VMEM((width * width, GROUP * 2 * site_count), jnp.bfloat16),
            pltpu.VMEM((2 * width * mom, width * width), jnp.float32),
        ],
        name="project",
    )(eps_rows, eps_sign, source_sites, momenta, slabs)

    moved = lax.all_to_all(partial_value, ("ta", "sa"), split_axis=0, concat_axis=0, tiled=True)
    moved = moved.reshape((lax.axis_size("ta"), lax.axis_size("sa")) + moved.shape[1:])
    summed = jnp.sum(moved, axis=1)
    summed = summed.reshape((lax.axis_size("ta"), src_count, time_count) + summed.shape[2:])
    summed = jnp.moveaxis(summed, 1, 0).reshape((src_count, -1) + summed.shape[3:])
    return lax.all_gather(summed, "src", axis=0, tiled=True)


def solution(mesh):
    return jax.shard_map(
        per_device,
        mesh=mesh,
        in_specs=(P(("cfg", "src"), "ta", None, None, None, "sa"), P(), P(), P("cfg", None), P()),
        out_specs=P("cfg", None, None, "ta", "sa"),
        check_vma=False,
    )
```

time: 325 us -> 31.1 us (0.10)
  local copies, waits for them, and re-layouts: 174 us -> 4.6 us
  matrix products: 86.5 us -> 0 us
  waiting for transfers between devices: 21.5 us -> 0 us
  other arithmetic: 15.3 us -> 0.09 us
  between operations: 13.5 us -> 0.02 us
  Pallas kernels: 0 us -> 8.41 us
  blocking collectives: 12.3 us -> 17.7 us
    dot_general x4 -> x0, matrix products: 86.5 us -> none  [the longest x2 82.4 us: contract(): jnp.einsum('ceijx,oceLx->oijLx', pair, mixer, preferred_element_type=jnp....]
    another operation x4 -> x1, local copies, waits for them, and re-layouts: 81.1 us -> 0.01 us  [per_device(): jnp.moveaxis(summed, 1, 0).reshape((src_count, -1) + summed.shape[3:])]
    convert_element_type x2 -> x0, local copies, waits for them, and re-layouts: 58.5 us -> none  [contract(): block.astype(jnp.bfloat16)]
    unnamed x2 -> x0, waiting for transfers between devices: 21.5 us -> none
    gather x6 -> x0, local copies, waits for them, and re-layouts: 8.66 us -> none  [the longest x2 4.1 us: contract(): third = jnp.take(slab, rows[:, 2], axis=1)]
    pallas_call x0 -> x1, Pallas kernels: none -> 8.41 us  [per_device(): pl.pallas_call(body, grid=(slabs.shape[0],), in_specs=[smem, smem, smem,...]
    unnamed x7 -> x5, local copies, waits for them, and re-layouts: 11.3 us -> 3.78 us
    all_to_all x1, blocking collectives: 10.3 us -> 15.7 us  [per_device(): lax.all_to_all(partial_value, ('ta', 'sa'), split_axis=0, concat_axis=0,...]
  transfers between devices with their start and end apart: 1 -> 0, of which waited for: 1 -> 0; matrix products, arithmetic and copies ran while one was open for 0% -> 0% of each run, Pallas kernels for 0% -> 0%
where the time goes in v1:
time: 31.1 us; the launch traced here: 30.8 us
  blocking collectives  17.7 us (57%)
  Pallas kernels  8.41 us (27%)
  local copies, waits for them, and re-layouts  4.6 us (15%)
    all_to_all x1, blocking collectives, per_device(): lax.all_to_all(partial_value, ('ta', 'sa'), split_axis=0, concat_axis=0,...  15.7 us
    pallas_call x1, Pallas kernels, per_device(): pl.pallas_call(body, grid=(slabs.shape[0],), in_specs=[smem, smem, smem,...  8.41 us
    unnamed x5, local copies, waits for them, and re-layouts  3.78 us
    all_gather x1, blocking collectives, per_device(): return lax.all_gather(summed, 'src', axis=0, tiled=True)  1.97 us
    all_gather x1, local copies, waits for them, and re-layouts, per_device(): return lax.all_gather(summed, 'src', axis=0, tiled=True)  0.81 us

profile of v1, /device:TPU:0, one launch (start us, length us, event | category | flops | bytes accessed | tf_op | source)
XLA Modules:
  0.0 30.8 jit_solution(13970060988871898661)
XLA Ops:
  0.0 0.0 copy-start
  0.0 1.4 %copy.15.refs_3_ = s32[8,3]{1,0:T(8,128)} copy(s32[8,3]{0,1:T(4,128)} %param.9) | data formatting | bytes 192 | tf_op args[4]
  1.4 0.0 copy-done
  1.4 0.7 %copy.14.refs_0_ = s32[24,3]{1,0:T(8,128)} copy(s32[24,3]{0,1:T(4,128)S(1)} %copy-done) | data formatting | bytes 576 | tf_op args[1]
  2.0 1.7 %copy.19 = bf16[1,2,2,12,12,256]{5,4,3,2,1,0:T(8,128)(2,1)} copy(bf16[1,2,2,12,12,256]{5,2,4,3,1,0:T(2,128)(2,1)} %param.5) | data formatting | bytes 589824 | tf_op args[0]
  3.8 8.4 %project.1 = f32[8,2,2,2,864]{4,3,2,1,0:T(2,128)} custom-call(s32[24,3]{1,0:T(8,128)} %copy.14.refs_0_, s32[24]{0:T(128)} %refs_1_.1, s32[2,3]{1,0:T(2,128)} %refs_2_.1, s32[8,3]{1,0:T(8,128)} %copy.15.refs_3_, bf16[2,2,12,12,256]{4,3,2,1,0:T(8,128)(2,1)} %bitcast.6), custom_call_target="tpu_custom_call" | custom-call | tf_op jit(solution)/shard_map/project/pallas_call | solution.py:139
  12.2 15.7 %all_to_all.5 = f32[8,2,2,2,864]{4,3,2,1,0:T(2,128)S(1)} all-to-all(f32[8,2,2,2,864]{4,3,2,1,0:T(2,128)} %project.1), channel_id=1, replica_groups=mesh['cfg'=2,'ta'=4,'sa'=2,'src'=2] {'ta','sa'}, dimensions={0} | all-to-all | bytes 442368 | tf_op jit(solution)/shard_map/all_to_all | solution.py:159
  27.9 0.1 bitcast_reduce_fusion
  28.0 2.0 %all_gather.3 = f32[2,8,2,2,864]{4,1,3,2,0:T(8,128)S(1)} all-gather(f32[1,8,2,2,864]{4,1,3,2,0:T(8,128)S(1)} %copy.16), channel_id=1, replica_groups=mesh['cfg'=2,'ta'=4,'sa'=2,'src'=2] {'src'}, dimensions={0}, use_global_device_ids=true | all-gather | bytes 331776 | tf_op jit(solution)/shard_map/all_gather | solution.py:164
  30.0 0.8 %copy.17 = f32[2,8,2,2,864]{4,3,2,1,0:T(2,128)} copy(f32[2,8,2,2,864]{4,1,3,2,0:T(8,128)S(1)} %all_gather.3) | data formatting | bytes 442368 | tf_op jit(solution)/shard_map/all_gather | solution.py:164
  (1 shorter events, 0.0 us)
Async XLA Ops:
  0.0 1.4 %copy-start = (s32[24,3]{0,1:T(4,128)S(1)}, s32[24,3]{0,1:T(4,128)}, u32[]{:S(2)}) copy-start(s32[24,3]{0,1:T(4,128)} %param.6) | copy-start | bytes 868

commit v2 on v1

--- a/solution.py
+++ b/solution.py
@@ -18,35 +18,41 @@
     return jnp.mod(value, length)
 
 
-def project_kernel(rows, signs, sites, momenta, prop, out, spread, tiled, phased, pairs, total, *,
+def project_kernel(rows, signs, sites, momenta, prop, out, spread, tiled, phased, pairs, total, table, *,
                    times, site_count, sites_total, scale):
     step = pl.program_id(0)
-    width = prop.shape[2]
-    mom = momenta.shape[0]
-    terms = rows.shape[0]
+    width = prop.shape[1]
+    mom = momenta.shape[1]
+    terms = rows.shape[1]
     extent_x = sites_total // (LY * LZ)
     per = mom * width
     square = width * width
 
-    owner = lax.axis_index("src") * (pl.num_programs(0) // times) + step // times
-    site = lax.axis_index("sa") * site_count + lax.broadcasted_iota(jnp.int32, (mom, site_count), 1)
-    coord_x = site // (LY * LZ)
-    coord_y = wrap(site // LZ, LY)
-    coord_z = wrap(site, LZ)
-    part_x = wrap(momenta[:, 0:1] * (coord_x - sites[owner, 0]), extent_x)
-    part_y = wrap(momenta[:, 1:2] * (coord_y - sites[owner, 1]), LY)
-    part_z = wrap(momenta[:, 2:3] * (coord_z - sites[owner, 2]), LZ)
-    angle = (2.0 * math.pi) * (
-        part_x.astype(jnp.float32) / extent_x
-        + part_y.astype(jnp.float32) / LY
-        + part_z.astype(jnp.float32) / LZ
-    )
-    cosine = jnp.cos(angle).astype(jnp.bfloat16).astype(jnp.float32)
-    sine = jnp.sin(angle).astype(jnp.bfloat16).astype(jnp.float32)
+    @pl.when(step % times == 0)
+    def _():
+        owner = lax.axis_index("src") * (pl.num_programs(0) // times) + step // times
+        site = lax.axis_index("sa") * site_count + lax.broadcasted_iota(jnp.int32, (mom, site_count), 1)
+        row = lax.broadcasted_iota(jnp.int32, (mom, site_count), 0)
+        coords = (site // (LY * LZ), wrap(site // LZ, LY), wrap(site, LZ))
+        lengths = (extent_x, LY, LZ)
+        turns = []
+        for d in range(3):
+            factor = jnp.zeros((mom, site_count), jnp.int32)
+            for p in range(mom):
+                factor = jnp.where(row == p, momenta[d, p], factor)
+            part = wrap(factor * (coords[d] - sites[owner, d]), lengths[d])
+            turns.append(part.astype(jnp.float32) / lengths[d])
+        angle = (2.0 * math.pi) * (turns[0] + turns[1] + turns[2])
+        table[0] = jnp.cos(angle).astype(jnp.bfloat16).astype(jnp.float32)
+        table[1] = jnp.sin(angle).astype(jnp.bfloat16).astype(jnp.float32)
+
+    cosine = table[0]
+    sine = table[1]
     low = lax.broadcasted_iota(jnp.int32, (8, site_count), 0) < 4
 
     def prepare(r, carry):
-        parts = [prop[0, c, r].astype(jnp.float32) for c in range(2)]
+        both = prop[0, r].astype(jnp.float32)
+        parts = [both[:, c] for c in range(2)]
         for c in range(2):
             tiled[r, c] = jnp.concatenate([parts[c], parts[c]], axis=0)
             for j in range(0, width, 2):
@@ -82,8 +88,8 @@
         left = []
         for u in range(GROUP):
             e = block * GROUP + u
-            r1 = rows[e, 1]
-            r2 = rows[e, 2]
+            r1 = rows[1, e]
+            r2 = rows[2, e]
             weight = (2 * signs[e] - 1).astype(jnp.float32)
             re2 = tiled[r2, 0] * weight
             im2 = tiled[r2, 1] * weight
@@ -97,7 +103,7 @@
                 pairs[j:j + 4 * width, at + site_count:at + 2 * site_count] = (
                     re1 * im2 + im1 * re2
                 ).astype(jnp.bfloat16)
-            left.append(phased[rows[e, 0]])
+            left.append(phased[rows[0, e]])
         total[...] += lax.dot_general(
             jnp.concatenate(left, axis=1), pairs[...], (((1,), (1,)), ((), ())),
             preferred_element_type=jnp.float32,
@@ -127,7 +133,8 @@
     mom = momenta.shape[0]
     terms = eps_rows.shape[0]
     scale = 1.0 / math.sqrt(4.0 * terms * sites_total)
-    slabs = prop.reshape((src_count * time_count,) + prop.shape[2:])
+    slabs = jnp.transpose(prop, (0, 1, 3, 4, 2, 5))
+    slabs = slabs.reshape((src_count * time_count,) + slabs.shape[2:])
     owners = lax.axis_size("ta") * lax.axis_size("sa")
     mine = mom // lax.axis_size("ta")
     span = width ** 3 // lax.axis_size("sa")
@@ -140,8 +147,7 @@
         body,
         grid=(slabs.shape[0],),
         in_specs=[
-            smem, smem, smem,
-            pl.BlockSpec(momenta.shape, lambda s: (0, 0)),
+            smem, smem, smem, smem,
             pl.BlockSpec((1,) + slabs.shape[1:], lambda s: (s, 0, 0, 0, 0)),
         ],
         out_specs=pl.BlockSpec((owners, 1, 2, mine, span), lambda s: (0, s, 0, 0, 0)),
@@ -152,9 +158,10 @@
             pltpu.VMEM((width, 2 * width * mom, 2 * site_count), jnp.bfloat16),
             pltpu.VMEM((width * width, GROUP * 2 * site_count), jnp.bfloat16),
             pltpu.VMEM((2 * width * mom, width * width), jnp.float32),
+            pltpu.VMEM((2, mom, site_count), jnp.float32),
         ],
         name="project",
-    )(eps_rows, eps_sign, source_sites, momenta, slabs)
+    )(eps_rows.T, eps_sign, source_sites, momenta.T, slabs)
 
     moved = lax.all_to_all(partial_value, ("ta", "sa"), split_axis=0, concat_axis=0, tiled=True)
     moved = moved.reshape((lax.axis_size("ta"), lax.axis_size("sa")) + moved.shape[1:])

time: 31.1 us -> 27.5 us (0.88)
  local copies, waits for them, and re-layouts: 4.6 us -> 0.82 us
    unnamed x5 -> x0, local copies, waits for them, and re-layouts: 3.78 us -> none
where the time goes in v2:
time: 27.5 us; the launch traced here: 27.2 us
  blocking collectives  17.7 us (64%)
  Pallas kernels  8.63 us (31%)
  local copies, waits for them, and re-layouts  0.82 us (3%)
    all_to_all x1, blocking collectives, per_device(): lax.all_to_all(partial_value, ('ta', 'sa'), split_axis=0, concat_axis=0,...  15.7 us
    pallas_call x1, Pallas kernels, per_device(): pl.pallas_call(body, grid=(slabs.shape[0],), in_specs=[smem, smem, smem,...  8.63 us
    all_gather x1, blocking collectives, per_device(): return lax.all_gather(summed, 'src', axis=0, tiled=True)  1.97 us
    all_gather x1, local copies, waits for them, and re-layouts, per_device(): return lax.all_gather(summed, 'src', axis=0, tiled=True)  0.81 us

profile of v2, /device:TPU:0, one launch (start us, length us, event | category | flops | bytes accessed | tf_op | source)
XLA Modules:
  0.0 27.2 jit_solution(4529512555299330349)
XLA Ops:
  0.0 8.6 %project.1 = f32[8,2,2,2,864]{4,3,2,1,0:T(2,128)} custom-call(s32[3,24]{1,0:T(4,128)} %bitcast.10, s32[24]{0:T(128)} %refs_1_.1, s32[2,3]{1,0:T(2,128)} %refs_2_.1, s32[3,8]{1,0:T(4,128)} %bitcast.11, bf16[2,12,12,2,256]{4,3,2,1,0:T(2,128)(2,1)} %bitcast.9), custom_call_target="tpu_custom_call" | custom-call | tf_op jit(solution)/shard_map/project/pallas_call | solution.py:146
  8.6 15.7 %all_to_all.5 = f32[8,2,2,2,864]{4,3,2,1,0:T(2,128)S(1)} all-to-all(f32[8,2,2,2,864]{4,3,2,1,0:T(2,128)} %project.1), channel_id=1, replica_groups=mesh['cfg'=2,'ta'=4,'sa'=2,'src'=2] {'ta','sa'}, dimensions={0} | all-to-all | bytes 442368 | tf_op jit(solution)/shard_map/all_to_all | solution.py:166
  24.3 0.1 bitcast_reduce_fusion
  24.4 2.0 %all_gather.3 = f32[2,8,2,2,864]{4,1,3,2,0:T(8,128)S(1)} all-gather(f32[1,8,2,2,864]{4,1,3,2,0:T(8,128)S(1)} %copy.7), channel_id=1, replica_groups=mesh['cfg'=2,'ta'=4,'sa'=2,'src'=2] {'src'}, dimensions={0}, use_global_device_ids=true | all-gather | bytes 331776 | tf_op jit(solution)/shard_map/all_gather | solution.py:171
  26.4 0.8 %copy.8 = f32[2,8,2,2,864]{4,3,2,1,0:T(2,128)} copy(f32[2,8,2,2,864]{4,1,3,2,0:T(8,128)S(1)} %all_gather.3) | data formatting | bytes 442368 | tf_op jit(solution)/shard_map/all_gather | solution.py:171
  (1 shorter events, 0.0 us)

commit v3 on v2

--- a/solution.py
+++ b/solution.py
@@ -18,7 +18,7 @@
     return jnp.mod(value, length)
 
 
-def project_kernel(rows, signs, sites, momenta, prop, out, spread, tiled, phased, pairs, total, table, *,
+def project_kernel(rows, signs, sites, momenta, prop, out, tiled, phased, pairs, total, table, *,
                    times, site_count, sites_total, scale):
     step = pl.program_id(0)
     width = prop.shape[1]
@@ -55,13 +55,6 @@
         parts = [both[:, c] for c in range(2)]
         for c in range(2):
             tiled[r, c] = jnp.concatenate([parts[c], parts[c]], axis=0)
-            for j in range(0, width, 2):
-                first = jnp.broadcast_to(parts[c][j:j + 1], (8, site_count))
-                second = jnp.broadcast_to(parts[c][j + 1:j + 2], (8, site_count))
-                at = j * width
-                spread[r, c, at:at + 8] = first
-                spread[r, c, at + 8:at + 16] = jnp.where(low, first, second)
-                spread[r, c, at + 16:at + 24] = second
         for i in range(0, width, 2):
             reals = []
             imags = []
@@ -93,16 +86,27 @@
             weight = (2 * signs[e] - 1).astype(jnp.float32)
             re2 = tiled[r2, 0] * weight
             im2 = tiled[r2, 1] * weight
-            re2 = jnp.concatenate([re2, re2], axis=0)
-            im2 = jnp.concatenate([im2, im2], axis=0)
             at = u * 2 * site_count
-            for j in range(0, square, 4 * width):
-                re1 = spread[r1, 0, j:j + 4 * width]
-                im1 = spread[r1, 1, j:j + 4 * width]
-                pairs[j:j + 4 * width, at:at + site_count] = (re1 * re2 - im1 * im2).astype(jnp.bfloat16)
-                pairs[j:j + 4 * width, at + site_count:at + 2 * site_count] = (
-                    re1 * im2 + im1 * re2
-                ).astype(jnp.bfloat16)
+            for j in range(0, width, 4):
+                reals = []
+                imags = []
+                for q in (j, j + 2):
+                    ends = [
+                        [tiled[r1, c, pl.ds(k, 8, stride=0)] for k in (q, q + 1)] for c in range(2)
+                    ]
+                    mixed = [jnp.where(low, ends[c][0], ends[c][1]) for c in range(2)]
+                    for v, (re1, im1) in enumerate(
+                        ((ends[0][0], ends[1][0]), (mixed[0], mixed[1]), (ends[0][1], ends[1][1]))
+                    ):
+                        re = re2[8 * v:8 * v + 8]
+                        im = im2[8 * v:8 * v + 8]
+                        reals.append(re1 * re - im1 * im)
+                        imags.append(re1 * im + im1 * re)
+                span = slice(j * width, (j + 4) * width)
+                pairs[span, at:at + site_count] = jnp.concatenate(reals, axis=0).astype(jnp.bfloat16)
+                pairs[span, at + site_count:at + 2 * site_count] = (
+                    jnp.concatenate(imags, axis=0).astype(jnp.bfloat16)
+                )
             left.append(phased[rows[0, e]])
         total[...] += lax.dot_general(
             jnp.concatenate(left, axis=1), pairs[...], (((1,), (1,)), ((), ())),
@@ -122,7 +126,7 @@
             half = i // span
             at = (i % span) * square
             for a in range(owners // halves):
-                out[a * halves + half, 0, c, :, at:at + square] = value[a * mine:(a + 1) * mine]
+                out[a * halves + half, step, c, :, at:at + square] = value[a * mine:(a + 1) * mine]
 
 
 def per_device(prop, eps_rows, eps_sign, source_sites, momenta):
@@ -150,10 +154,9 @@
             smem, smem, smem, smem,
             pl.BlockSpec((1,) + slabs.shape[1:], lambda s: (s, 0, 0, 0, 0)),
         ],
-        out_specs=pl.BlockSpec((owners, 1, 2, mine, span), lambda s: (0, s, 0, 0, 0)),
-        out_shape=jax.ShapeDtypeStruct((owners, slabs.shape[0], 2, mine, span), jnp.float32),
+        out_specs=pl.BlockSpec(memory_space=pltpu.VMEM),
+        out_shape=pltpu.VMEM((owners, slabs.shape[0], 2, mine, span), jnp.float32),
         scratch_shapes=[
-            pltpu.VMEM((width, 2, width * width, site_count), jnp.float32),
             pltpu.VMEM((width, 2, 2 * width, site_count), jnp.float32),
             pltpu.VMEM((width, 2 * width * mom, 2 * site_count), jnp.bfloat16),
             pltpu.VMEM((width * width, GROUP * 2 * site_count), jnp.bfloat16),

time: 27.5 us -> 26.3 us (0.956)
  Pallas kernels: 8.63 us -> 7.72 us
    pallas_call x1, Pallas kernels: 8.63 us -> 7.72 us  [per_device(): pl.pallas_call(body, grid=(slabs.shape[0],), in_specs=[smem, smem, smem,...]
where the time goes in v3:
time: 26.3 us; the launch traced here: 26.1 us
  blocking collectives  17.5 us (67%)
  Pallas kernels  7.72 us (29%)
  local copies, waits for them, and re-layouts  0.82 us (3%)
    all_to_all x1, blocking collectives, per_device(): lax.all_to_all(partial_value, ('ta', 'sa'), split_axis=0, concat_axis=0,...  15.5 us
    pallas_call x1, Pallas kernels, per_device(): pl.pallas_call(body, grid=(slabs.shape[0],), in_specs=[smem, smem, smem,...  7.72 us
    all_gather x1, blocking collectives, per_device(): return lax.all_gather(summed, 'src', axis=0, tiled=True)  1.97 us
    all_gather x1, local copies, waits for them, and re-layouts, per_device(): return lax.all_gather(summed, 'src', axis=0, tiled=True)  0.81 us

profile of v3, /device:TPU:0, one launch (start us, length us, event | category | flops | bytes accessed | tf_op | source)
XLA Modules:
  0.0 26.1 jit_solution(3526302089945983767)
XLA Ops:
  0.0 7.7 %project.1 = f32[8,2,2,2,864]{4,3,2,1,0:T(2,128)S(1)} custom-call(s32[3,24]{1,0:T(4,128)} %bitcast.10, s32[24]{0:T(128)} %refs_1_.1, s32[2,3]{1,0:T(2,128)} %refs_2_.1, s32[3,8]{1,0:T(4,128)} %bitcast.11, bf16[2,12,12,2,256]{4,3,2,1,0:T(2,128)(2,1)} %bitcast.9), custom_call_target="tpu_custom_call" | custom-call | tf_op jit(solution)/shard_map/project/pallas_call | solution.py:150
  7.7 15.5 %all_to_all.5 = f32[8,2,2,2,864]{4,3,2,1,0:T(2,128)S(1)} all-to-all(f32[8,2,2,2,864]{4,3,2,1,0:T(2,128)S(1)} %project.1), channel_id=1, replica_groups=mesh['cfg'=2,'ta'=4,'sa'=2,'src'=2] {'ta','sa'}, dimensions={0} | all-to-all | bytes 442368 | tf_op jit(solution)/shard_map/all_to_all | solution.py:169
  23.2 0.1 bitcast_reduce_fusion
  23.4 2.0 %all_gather.3 = f32[2,8,2,2,864]{4,1,3,2,0:T(8,128)S(1)} all-gather(f32[1,8,2,2,864]{4,1,3,2,0:T(8,128)S(1)} %copy.7), channel_id=1, replica_groups=mesh['cfg'=2,'ta'=4,'sa'=2,'src'=2] {'src'}, dimensions={0}, use_global_device_ids=true | all-gather | bytes 331776 | tf_op jit(solution)/shard_map/all_gather | solution.py:174
  25.3 0.8 %copy.8 = f32[2,8,2,2,864]{4,3,2,1,0:T(2,128)} copy(f32[2,8,2,2,864]{4,1,3,2,0:T(8,128)S(1)} %all_gather.3) | data formatting | bytes 442368 | tf_op jit(solution)/shard_map/all_gather | solution.py:174
  (1 shorter events, 0.0 us)

commit v4 on v3

--- a/solution.py
+++ b/solution.py
@@ -9,7 +9,7 @@
 
 LY = 16
 LZ = 16
-GROUP = 4
+GROUP = 24
 
 
 def wrap(value, length):
@@ -75,12 +75,12 @@
         return carry
 
     lax.fori_loop(0, width, prepare, 0)
-    total[...] = jnp.zeros_like(total)
+    group = max(g for g in range(1, GROUP + 1) if terms % g == 0)
 
     def accumulate(block, carry):
         left = []
-        for u in range(GROUP):
-            e = block * GROUP + u
+        for u in range(group):
+            e = block * group + u
             r1 = rows[1, e]
             r2 = rows[2, e]
             weight = (2 * signs[e] - 1).astype(jnp.float32)
@@ -108,13 +108,21 @@
                     jnp.concatenate(imags, axis=0).astype(jnp.bfloat16)
                 )
             left.append(phased[rows[0, e]])
-        total[...] += lax.dot_general(
-            jnp.concatenate(left, axis=1), pairs[...], (((1,), (1,)), ((), ())),
+        product = lax.dot_general(
+            jnp.concatenate(left, axis=1), pairs[:, :group * 2 * site_count], (((1,), (1,)), ((), ())),
             preferred_element_type=jnp.float32,
         )
+        if terms == group:
+            total[...] = product
+        else:
+            total[...] += product
         return carry
 
-    lax.fori_loop(0, terms // GROUP, accumulate, 0)
+    if terms == group:
+        accumulate(0, 0)
+    else:
+        total[...] = jnp.zeros_like(total)
+        lax.fori_loop(0, terms // group, accumulate, 0)
 
     owners = out.shape[0]
     mine = out.shape[3]
@@ -159,7 +167,7 @@
         scratch_shapes=[
             pltpu.VMEM((width, 2, 2 * width, site_count), jnp.float32),
             pltpu.VMEM((width, 2 * width * mom, 2 * site_count), jnp.bfloat16),
-            pltpu.VMEM((width * width, GROUP * 2 * site_count), jnp.bfloat16),
+            pltpu.VMEM((width * width, min(GROUP, terms) * 2 * site_count), jnp.bfloat16),
             pltpu.VMEM((2 * width * mom, width * width), jnp.float32),
             pltpu.VMEM((2, mom, site_count), jnp.float32),
         ],

time: 26.3 us -> 24.2 us (0.920)
  Pallas kernels: 7.72 us -> 5.59 us
    pallas_call x1, Pallas kernels: 7.72 us -> 5.59 us  [per_device(): pl.pallas_call(body, grid=(slabs.shape[0],), in_specs=[smem, smem, smem,...]
where the time goes in v4:
time: 24.2 us; the launch traced here: 24 us
  blocking collectives  17.5 us (72%)
  Pallas kernels  5.59 us (23%)
  local copies, waits for them, and re-layouts  0.82 us (3%)
    all_to_all x1, blocking collectives, per_device(): lax.all_to_all(partial_value, ('ta', 'sa'), split_axis=0, concat_axis=0,...  15.5 us
    pallas_call x1, Pallas kernels, per_device(): pl.pallas_call(body, grid=(slabs.shape[0],), in_specs=[smem, smem, smem,...  5.59 us
    all_gather x1, blocking collectives, per_device(): return lax.all_gather(summed, 'src', axis=0, tiled=True)  1.97 us
    all_gather x1, local copies, waits for them, and re-layouts, per_device(): return lax.all_gather(summed, 'src', axis=0, tiled=True)  0.81 us

profile of v4, /device:TPU:0, one launch (start us, length us, event | category | flops | bytes accessed | tf_op | source)
XLA Modules:
  0.0 24.0 jit_solution(11298981793127579921)
XLA Ops:
  0.0 5.6 %project.1 = f32[8,2,2,2,864]{4,3,2,1,0:T(2,128)S(1)} custom-call(s32[3,24]{1,0:T(4,128)} %bitcast.10, s32[24]{0:T(128)} %refs_1_.1, s32[2,3]{1,0:T(2,128)} %refs_2_.1, s32[3,8]{1,0:T(4,128)} %bitcast.11, bf16[2,12,12,2,256]{4,3,2,1,0:T(2,128)(2,1)} %bitcast.9), custom_call_target="tpu_custom_call" | custom-call | tf_op jit(solution)/shard_map/project/pallas_call | solution.py:158
  5.6 15.5 %all_to_all.5 = f32[8,2,2,2,864]{4,3,2,1,0:T(2,128)S(1)} all-to-all(f32[8,2,2,2,864]{4,3,2,1,0:T(2,128)S(1)} %project.1), channel_id=1, replica_groups=mesh['cfg'=2,'ta'=4,'sa'=2,'src'=2] {'ta','sa'}, dimensions={0} | all-to-all | bytes 442368 | tf_op jit(solution)/shard_map/all_to_all | solution.py:177
  21.1 0.1 bitcast_reduce_fusion
  21.2 2.0 %all_gather.3 = f32[2,8,2,2,864]{4,1,3,2,0:T(8,128)S(1)} all-gather(f32[1,8,2,2,864]{4,1,3,2,0:T(8,128)S(1)} %copy.7), channel_id=1, replica_groups=mesh['cfg'=2,'ta'=4,'sa'=2,'src'=2] {'src'}, dimensions={0}, use_global_device_ids=true | all-gather | bytes 331776 | tf_op jit(solution)/shard_map/all_gather | solution.py:182
  23.2 0.8 %copy.8 = f32[2,8,2,2,864]{4,3,2,1,0:T(2,128)} copy(f32[2,8,2,2,864]{4,1,3,2,0:T(8,128)S(1)} %all_gather.3) | data formatting | bytes 442368 | tf_op jit(solution)/shard_map/all_gather | solution.py:182
  (1 shorter events, 0.0 us)
